TPU v7x, 128 devices: a whole 4x4x4 slice. The times are simulated.
128 devices in a mesh: seq: 8 (over z, core), grp: 16 (over y, x).
Axes of the slice: x: 4, y: 4, z: 4, core: 2. Of those that a mesh axis runs over, the one named last changes fastest.
Arguments:
- hidden_in: bfloat16 [16, 4096, 1024], P('grp', 'seq'), may hold values from -64 to 64, as said below
- lengths: int32 [16], P('grp'), may hold values from 512 to 4096
- project_weight: bfloat16 [1024, 3072], replicated, may hold values from -0.1875 to 0.1875
- output_weight: bfloat16 [1024, 1024], replicated, may hold values from -0.1875 to 0.1875
- first_gain: float32 [1024], replicated, may hold values from 0.5 to 1.5
- first_shift: float32 [1024], replicated, may hold values from -3 to 3
- up_weight: bfloat16 [1024, 4096], P('grp'), may hold values from -0.1875 to 0.1875
- down_weight: bfloat16 [1024, 4096], P('grp'), may hold values from -0.09375 to 0.09375
- second_gain: float32 [1024], replicated, may hold values from 0.5 to 1.5
- second_shift: float32 [1024], replicated, may hold values from -3 to 3
- queries: float32 [128, 1024], P('grp'), may hold values from -6 to 6
- positive: int32 [128], P('grp'), may hold values from 0 to 15
Outputs:
- hidden_out: bfloat16 [16, 4096, 1024], P('grp', 'seq')
- embeddings: float32 [16, 1024], P('grp')
- query_loss: float32 [128], P('grp')
Inputs may be any that keep to these rules, and one draw needn't show every extreme that they name: `hidden_in`: activations.
All inputs are finite; a program needn't handle non-finite values.
Results may differ from a plain program's by a relative error of at most 0.0076.
Values may be sent and summed in bfloat16 or wider, within the bound.
A program may use at most 192 MiB of HBM per device.

v0:
```python
import math
import jax
import jax.numpy as jnp
from jax import lax
from jax.sharding import PartitionSpec as P

HEAD_DIM = 64


def sent_together(arrays, axis, dim, along):
    widths = [a.shape[along] for a in arrays]
    both = jnp.concatenate(arrays, axis=along)
    result = lax.all_gather(both, axis, axis=dim, tiled=True)
    return tuple(jnp.split(result, [sum(widths[:k]) for k in range(1, len(widths))], axis=along))


def split_up(array, dim, devices):
    before, after = (array.shape[:dim], array.shape[dim + 1 :])
    return jnp.moveaxis(array.reshape(*before, devices, -1, *after), dim, 0)


def cut_rows(length, count):
    unit = 8 if length >= 8 * count else 1
    return [length // unit * k // count * unit for k in range(1, count)]


def laid_out(parts, dim):
    lengths = list(parts.shape[1:])
    lengths[dim] *= parts.shape[0]
    return jnp.moveaxis(parts, 0, dim).reshape(lengths)


def several_exchanges(array, axis, pieces, split_dim, concat_dim):
    parts = split_up(array, split_dim, lax.axis_size(axis))
    cut = max(range(1, max(2, parts.ndim - 1)), key=lambda d: parts.shape[d])
    outs = []
    for slab in jnp.split(parts, cut_rows(parts.shape[cut], pieces), axis=cut):
        if slab.size:
            outs.append(lax.all_to_all(slab, axis, split_axis=0, concat_axis=0, tiled=True))
    return laid_out(jnp.concatenate(outs, axis=cut), concat_dim)


def sent_to_all(array, axis):
    copies = jnp.broadcast_to(array, (lax.axis_size(axis), *array.shape))
    return lax.all_to_all(copies, axis, split_axis=0, concat_axis=0, tiled=True)


def taken_together(array, axis):
    everything = sent_to_all(array, axis)
    return jnp.sum(everything, axis=0)


def collect(array, axis, dim):
    parts = sent_to_all(array, axis)
    return laid_out(parts, dim)


def layer_norm(values, gain, shift):
    average = jnp.mean(values, axis=-1, keepdims=True)
    centred = values - average
    variance = jnp.mean(centred * centred, axis=-1, keepdims=True)
    return centred * lax.rsqrt(variance + 1e-05) * gain + shift


def attend_local(gathered, length):
    seq_len = gathered.shape[0]
    local_width = gathered.shape[2]
    head_count = local_width // HEAD_DIM
    block = min(1024, seq_len)
    query_all = gathered[:, 0, :].reshape(seq_len, head_count, HEAD_DIM)
    key_all = gathered[:, 1, :].reshape(seq_len, head_count, HEAD_DIM)
    value_all = gathered[:, 2, :].reshape(seq_len, head_count, HEAD_DIM)
    key_valid = jnp.arange(seq_len, dtype=jnp.int32) < length
    scale = 1.0 / math.sqrt(HEAD_DIM)

    def one_block(index):
        query_rows = lax.dynamic_slice_in_dim(query_all, index * block, block, 0)
        scores = (
            jnp.einsum("qhd,khd->hqk", query_rows, key_all, preferred_element_type=jnp.float32)
            * scale
        )
        scores = jnp.where(key_valid[None, None, :], scores, -jnp.inf)
        highest = jnp.max(scores, axis=-1, keepdims=True)
        expo = jnp.exp(scores - highest)
        probs = (expo / jnp.sum(expo, axis=-1, keepdims=True)).astype(jnp.bfloat16)
        result = jnp.einsum("hqk,khd->qhd", probs, value_all, preferred_element_type=jnp.float32)
        return result.astype(jnp.bfloat16).reshape(block, local_width)

    blocks = lax.map(one_block, jnp.arange(seq_len // block, dtype=jnp.int32))
    return blocks.reshape(seq_len, local_width)


def group_weights(up_part, down_part):
    return sent_together((up_part, down_part), "grp", 0, 1)


def expand_inner(rows_in, up_full):
    return jax.nn.gelu(
        jnp.dot(rows_in, up_full, preferred_element_type=jnp.float32), approximate=False
    ).astype(jnp.bfloat16)


def contract_down(inner_rows, down_full):
    return lax.dot_general(
        inner_rows, down_full, (((1,), (1,)), ((), ())), preferred_element_type=jnp.float32
    )


def body(
    hidden_in,
    lengths,
    project_weight,
    output_weight,
    first_gain,
    first_shift,
    up_weight,
    down_weight,
    second_gain,
    second_shift,
    queries,
    positive,
):
    tokens = hidden_in[0]
    tok_rows = tokens.shape[0]
    width = tokens.shape[1]
    rank = lax.axis_index("seq")
    length = lengths[0]
    projected = jnp.dot(tokens, project_weight, preferred_element_type=jnp.float32).astype(
        jnp.bfloat16
    )
    projected = projected.reshape(tok_rows, 3, width)
    gathered = several_exchanges(projected, "seq", 2, 2, 0)
    attended = attend_local(gathered, length)
    returned = lax.all_to_all(attended, "seq", split_axis=0, concat_axis=1, tiled=True)
    mixed = jnp.dot(returned, output_weight, preferred_element_type=jnp.float32)
    mixed = mixed + tokens.astype(jnp.float32)
    normed = layer_norm(mixed, first_gain, first_shift).astype(jnp.bfloat16)
    up_full, down_full = group_weights(up_weight, down_weight)
    inner = expand_inner(normed, up_full)
    outer = contract_down(inner, down_full)
    final = layer_norm(outer + normed.astype(jnp.float32), second_gain, second_shift)
    position = rank * tok_rows + jnp.arange(tok_rows, dtype=jnp.int32)
    valid = (position < length).astype(jnp.float32)
    local_total = jnp.sum(final * valid[:, None], axis=0)
    passage_total = taken_together(local_total, "seq")
    pooled = passage_total / length.astype(jnp.float32)
    embedding = pooled / jnp.sqrt(jnp.sum(pooled * pooled) + 1e-06)
    short_passages = collect(embedding.astype(jnp.bfloat16)[None, :], "grp", 0)
    short_queries = (
        queries / jnp.sqrt(jnp.sum(queries * queries, axis=-1, keepdims=True) + 1e-06)
    ).astype(jnp.bfloat16)
    logits = 20.0 * jnp.dot(short_queries, short_passages.T, preferred_element_type=jnp.float32)
    passage_ids = jnp.arange(short_passages.shape[0], dtype=jnp.int32)
    chosen = positive[:, None] == passage_ids[None, :]
    picked = jnp.sum(jnp.where(chosen, logits, 0.0), axis=1)
    query_loss = jnp.log(jnp.sum(jnp.exp(logits), axis=1)) - picked
    return (final.astype(jnp.bfloat16)[None], embedding[None, :], query_loss)


def solution(mesh):
    in_specs = (
        P("grp", "seq", None),
        P("grp"),
        P(),
        P(),
        P(),
        P(),
        P("grp", None),
        P("grp", None),
        P(),
        P(),
        P("grp", None),
        P("grp"),
    )
    out_specs = (P("grp", "seq", None), P("grp", None), P("grp"))
    return jax.shard_map(body, mesh=mesh, in_specs=in_specs, out_specs=out_specs, check_vma=False)
```

profile of v0, /device:TPU:0, one launch (start us, length us, event | category | flops | bytes accessed | tf_op | source)
XLA Modules:
  0.0 313.7 jit_solution(6332534830161004990)
XLA Ops:
  7.2 2.4 pad_maximum_fusion.1
  9.6 6.6 %fusion.69 = bf16[64,8,24,128]{3,1,2,0:T(8,128)(2,1)S(1)} fusion(bf16[1024,3072]{1,0:T(8,128)(2,1)} %param.16, bf16[1,512,1024]{2,1,0:T(8,128)(2,1)} %param.14), kind=kOutput, calls=%fused_computation.84 | convolution fusion | flops 3222798336 | bytes 10485760 | tf_op jit(solution)/shard_map/dot_general | solution.py:128
  17.7 1.5 fusion.130
  19.3 26.9 %all_to_all.40 = bf16[8,256,3,128]{3,1,2,0:T(8,128)(2,1)} all-to-all(bf16[8,256,3,128]{3,1,2,0:T(8,128)(2,1)S(1)} %get-tuple-element.88), channel_id=1, replica_groups=mesh['seq'=8,'grp'=16] {'seq'}, dimensions={0} | all-to-all | bytes 3145728 | tf_op jit(solution)/shard_map/all_to_all | solution.py:39
  46.2 4.5 %all-to-all-start.1 = ((bf16[8,256,3,128]{3,1,2,0:T(8,128)(2,1)}), bf16[8,256,3,128]{3,1,2,0:T(8,128)(2,1)}, u32[]{:S(2)}, u32[]{:S(2)}) async-start(bf16[8,256,3,128]{3,1,2,0:T(8,128)(2,1)} %get-tuple-element.89), calls=%async_computation.1 | async-start | bytes 3145728 | tf_op jit(solution)/shard_map/all_to_all | solution.py:39
  50.6 21.4 %all-to-all-done.1 = bf16[8,256,3,128]{3,1,2,0:T(8,128)(2,1)} async-done(((bf16[8,256,3,128]{3,1,2,0:T(8,128)(2,1)}), bf16[8,256,3,128]{3,1,2,0:T(8,128)(2,1)}, u32[]{:S(2)}, u32[]{:S(2)}) %all-to-all-start.1) | async-done | bytes 1572896 | tf_op jit(solution)/shard_map/all_to_all | solution.py:39
  72.0 2.2 pad_maximum_fusion
  74.5 1.6 fusion.129
  76.1 2.3 copy.46
  78.4 2.3 copy.47
  80.7 1.3 copy.48
  82.0 134.7 %while.11 = (s32[]{:T(128)}, bf16[4,1024,128]{2,1,0:T(8,128)(2,1)}, s32[4]{0:T(128)S(1)}, bf16[4096,2,64]{0,2,1:T(8,128)(2,1)}, bf16[4096,2,64]{0,2,1:T(8,128)(2...) while((s32[]{:T(128)}, bf16[4,1024,128]{2,1,0:T(8,128)(2,1)}, ...), condition=%wide.region_3.4_spmd.clone, body=%wide.region_0.3_spmd.clone.sunk | while | flops 2197954560 | bytes 70804144 | solution.py:89
  83.9 17.5 %fusion.154 = (f32[2,1024]{1,0:T(2,128)S(1)}, f32[2,1024,4096]{2,1,0:T(8,128)}) fusion(pred[4096]{0:T(1024)(128)(4,1)S(1)} %iota_compare_fusion.3, bf16[4096,2,64]{0,2,1:T(8,128)(2,1)} %get-tuple-element.169, bf16[4096,2,64]{0,2,1:T(8,128)(2,1)} %get-tuple-element.168, s32[]{:T(128)S(6)} %select_n.28), kind=kOutput, calls=%fused_computation.143.clone.1 | convolution fusion | flops 1107300352 | bytes 34877444 | tf_op jit(solution)/shard_map/while/body/eval_jaxpr/sub | solution.py:84
  101.4 13.9 %fusion.155 = bf16[2,1024,64]{1,2,0:T(8,128)(2,1)S(1)} fusion(bf16[4096,2,64]{0,2,1:T(8,128)(2,1)} %get-tuple-element.170, f32[2,1024,4096]{2,1,0:T(8,128)} %get-tuple-element.141, f32[2,1024]{1,0:T(2,128)S(1)} %get-tuple-element.142), kind=kOutput, calls=%fused_computation.11.clone.1 | convolution fusion | flops 1090650112 | bytes 34873344 | tf_op jit(solution)/shard_map/while/body/eval_jaxpr/hqk,khd->qhd/dot_general | solution.py:86
  118.1 17.1 %fusion.154 = (f32[2,1024]{1,0:T(2,128)S(1)}, f32[2,1024,4096]{2,1,0:T(8,128)}) fusion(pred[4096]{0:T(1024)(128)(4,1)S(1)} %iota_compare_fusion.3, bf16[4096,2,64]{0,2,1:T(8,128)(2,1)} %get-tuple-element.169, bf16[4096,2,64]{0,2,1:T(8,128)(2,1)} %get-tuple-element.168, s32[]{:T(128)S(6)} %select_n.28), kind=kOutput, calls=%fused_computation.143.clone.1 | convolution fusion | flops 1107300352 | bytes 34877444 | tf_op jit(solution)/shard_map/while/body/eval_jaxpr/sub | solution.py:84
  135.2 13.6 %fusion.155 = bf16[2,1024,64]{1,2,0:T(8,128)(2,1)S(1)} fusion(bf16[4096,2,64]{0,2,1:T(8,128)(2,1)} %get-tuple-element.170, f32[2,1024,4096]{2,1,0:T(8,128)} %get-tuple-element.141, f32[2,1024]{1,0:T(2,128)S(1)} %get-tuple-element.142), kind=kOutput, calls=%fused_computation.11.clone.1 | convolution fusion | flops 1090650112 | bytes 34873344 | tf_op jit(solution)/shard_map/while/body/eval_jaxpr/hqk,khd->qhd/dot_general | solution.py:86
  151.6 17.1 %fusion.154 = (f32[2,1024]{1,0:T(2,128)S(1)}, f32[2,1024,4096]{2,1,0:T(8,128)}) fusion(pred[4096]{0:T(1024)(128)(4,1)S(1)} %iota_compare_fusion.3, bf16[4096,2,64]{0,2,1:T(8,128)(2,1)} %get-tuple-element.169, bf16[4096,2,64]{0,2,1:T(8,128)(2,1)} %get-tuple-element.168, s32[]{:T(128)S(6)} %select_n.28), kind=kOutput, calls=%fused_computation.143.clone.1 | convolution fusion | flops 1107300352 | bytes 34877444 | tf_op jit(solution)/shard_map/while/body/eval_jaxpr/sub | solution.py:84
  168.7 13.6 %fusion.155 = bf16[2,1024,64]{1,2,0:T(8,128)(2,1)S(1)} fusion(bf16[4096,2,64]{0,2,1:T(8,128)(2,1)} %get-tuple-element.170, f32[2,1024,4096]{2,1,0:T(8,128)} %get-tuple-element.141, f32[2,1024]{1,0:T(2,128)S(1)} %get-tuple-element.142), kind=kOutput, calls=%fused_computation.11.clone.1 | convolution fusion | flops 1090650112 | bytes 34873344 | tf_op jit(solution)/shard_map/while/body/eval_jaxpr/hqk,khd->qhd/dot_general | solution.py:86
  185.1 17.1 %fusion.154 = (f32[2,1024]{1,0:T(2,128)S(1)}, f32[2,1024,4096]{2,1,0:T(8,128)}) fusion(pred[4096]{0:T(1024)(128)(4,1)S(1)} %iota_compare_fusion.3, bf16[4096,2,64]{0,2,1:T(8,128)(2,1)} %get-tuple-element.169, bf16[4096,2,64]{0,2,1:T(8,128)(2,1)} %get-tuple-element.168, s32[]{:T(128)S(6)} %select_n.28), kind=kOutput, calls=%fused_computation.143.clone.1 | convolution fusion | flops 1107300352 | bytes 34877444 | tf_op jit(solution)/shard_map/while/body/eval_jaxpr/sub | solution.py:84
  202.2 13.6 %fusion.155 = bf16[2,1024,64]{1,2,0:T(8,128)(2,1)S(1)} fusion(bf16[4096,2,64]{0,2,1:T(8,128)(2,1)} %get-tuple-element.170, f32[2,1024,4096]{2,1,0:T(8,128)} %get-tuple-element.141, f32[2,1024]{1,0:T(2,128)S(1)} %get-tuple-element.142), kind=kOutput, calls=%fused_computation.11.clone.1 | convolution fusion | flops 1090650112 | bytes 34873344 | tf_op jit(solution)/shard_map/while/body/eval_jaxpr/hqk,khd->qhd/dot_general | solution.py:86
  216.7 3.7 %all-to-all-start.2 = ((bf16[8,512,128]{2,1,0:T(8,128)(2,1)}), bf16[8,512,128]{2,1,0:T(8,128)(2,1)S(1)}, u32[]{:S(2)}, u32[]{:S(2)}) async-start(bf16[8,512,128]{2,1,0:T(8,128)(2,1)} %bitcast.57), calls=%async_computation.2 | async-start | bytes 2097152 | tf_op jit(solution)/shard_map/all_to_all | solution.py:134
  221.1 15.2 %all-to-all-done.2 = bf16[8,512,128]{2,1,0:T(8,128)(2,1)S(1)} async-done(((bf16[8,512,128]{2,1,0:T(8,128)(2,1)}), bf16[8,512,128]{2,1,0:T(8,128)(2,1)S(1)}, u32[]{:S(2)}, u32[]{:S(2)}) %all-to-all-start.2) | async-done | bytes 1048608 | tf_op jit(solution)/shard_map/all_to_all | solution.py:134
  236.3 1.3 copy.50
  237.6 2.9 fusion.131
  240.5 1.3 copy-done.1
  242.3 26.0 %fusion.73.clone.5 = bf16[512,4096]{1,0:T(8,128)(2,1)S(1)} fusion(bf16[1024,8192]{1,0:T(8,128)(2,1)} %all-gather.2.cloned.1.call-done, f32[512,1024]{1,0:T(8,128)} %copy-done.1, f32[1024]{0:T(1024)S(1)} %copy-done.6, f32[1024]{0:T(1024)S(1)} %copy-done.7, f32[512]{0:T(512)S(1)} %add_rsqrt_fusion.1, ...), kind=kOutput, calls=%fused_computation.24.clone.clone.clone.clone.clone.clone.2 | convolution fusion | flops 4433903616 | bytes 14692352 | tf_op jit(solution)/shard_map/dot_general | solution.py:99
  268.3 7.9 %fusion.132 = (f32[512]{0:T(512)S(1)}, f32[512,1024]{1,0:T(8,128)S(1)}) fusion(f32[1024]{0:T(1024)S(1)} %copy-done.6, f32[1024]{0:T(1024)S(1)} %copy-done.7, f32[512]{0:T(512)S(1)} %add_rsqrt_fusion.1, f32[512,1024]{1,0:T(8,128)S(1)} %copy-done.2, f32[512]{0:T(512)S(1)} %broadcast_multiply_fusion.1, bf16[1024,8192]{1,0:T(8,128)(2,1)} %all-gather.2.cloned.1.call-done, ...), kind=kOutput, calls=%fused_computation.147 | convolution fusion | flops 4299161088 | bytes 16791552 | tf_op jit(solution)/shard_map/dot_general | solution.py:104
  276.6 1.5 multiply_reduce_fusion
  278.7 3.3 %all-to-all-start.3 = ((f32[8,1,1024]{2,1,0:T(1,128)}), f32[8,1,1024]{2,1,0:T(1,128)S(1)}, u32[]{:S(2)}, u32[]{:S(2)}) async-start(f32[8,1,1024]{2,1,0:T(1,128)} %broadcast_in_dim.32), calls=%async_computation.3 | async-start | bytes 65536 | tf_op jit(solution)/shard_map/all_to_all | solution.py:45
  282.2 5.2 %all-to-all-done.3 = f32[8,1,1024]{2,1,0:T(1,128)S(1)} async-done(((f32[8,1,1024]{2,1,0:T(1,128)}), f32[8,1,1024]{2,1,0:T(1,128)S(1)}, u32[]{:S(2)}, u32[]{:S(2)}) %all-to-all-start.3) | async-done | bytes 32800 | tf_op jit(solution)/shard_map/all_to_all | solution.py:45
  291.4 6.9 %all-to-all-start.4 = ((bf16[16,2,512]{2,1,0:T(2,128)(2,1)}), bf16[16,2,512]{2,1,0:T(2,128)(2,1)S(1)}, u32[]{:S(2)}, u32[]{:S(2)}) async-start(bf16[16,2,512]{2,1,0:T(2,128)(2,1)} %reshape.80), calls=%async_computation.4 | async-start | bytes 65536 | tf_op jit(solution)/shard_map/all_to_all | solution.py:45
  298.3 7.6 %all-to-all-done.4 = bf16[16,2,512]{2,1,0:T(2,128)(2,1)S(1)} async-done(((bf16[16,2,512]{2,1,0:T(2,128)(2,1)}), bf16[16,2,512]{2,1,0:T(2,128)(2,1)S(1)}, u32[]{:S(2)}, u32[]{:S(2)}) %all-to-all-start.4) | async-done | bytes 32800 | tf_op jit(solution)/shard_map/all_to_all | solution.py:45
  (61 shorter events, 16.1 us)
Async XLA Ops:
  7.2 230.4 %copy-start = (bf16[1024,1024]{1,0:T(8,128)(2,1)S(1)}, bf16[1024,1024]{1,0:T(8,128)(2,1)}, u32[]{:S(2)}) copy-start(bf16[1024,1024]{1,0:T(8,128)(2,1)} %param.17) | copy-start | bytes 6291460
  7.2 235.0 %all-gather.2.cloned.1.call-start = ((), (), s32[]{:S(2)}) async-start(), calls=%async_computation.5 | async-start | bytes 17825792 | tf_op jit(solution)/shard_map/all_gather | solution.py:13
  46.2 25.9 %all-to-all-start.1 = ((bf16[8,256,3,128]{3,1,2,0:T(8,128)(2,1)}), bf16[8,256,3,128]{3,1,2,0:T(8,128)(2,1)}, u32[]{:S(2)}, u32[]{:S(2)}) async-start(bf16[8,256,3,128]{3,1,2,0:T(8,128)(2,1)} %get-tuple-element.89), calls=%async_computation.1 | async-start | bytes 3145728 | tf_op jit(solution)/shard_map/all_to_all | solution.py:39
  216.7 25.5 %copy-start.6 = (f32[1024]{0:T(1024)S(1)}, f32[1024]{0:T(1024)}, u32[]{:S(2)}) copy-start(f32[1024]{0:T(1024)} %param.19) | copy-start | bytes 12292
  216.7 25.5 %copy-start.7 = (f32[1024]{0:T(1024)S(1)}, f32[1024]{0:T(1024)}, u32[]{:S(2)}) copy-start(f32[1024]{0:T(1024)} %param.18) | copy-start | bytes 12292
  216.7 19.6 %all-to-all-start.2 = ((bf16[8,512,128]{2,1,0:T(8,128)(2,1)}), bf16[8,512,128]{2,1,0:T(8,128)(2,1)S(1)}, u32[]{:S(2)}, u32[]{:S(2)}) async-start(bf16[8,512,128]{2,1,0:T(8,128)(2,1)} %bitcast.57), calls=%async_computation.2 | async-start | bytes 2097152 | tf_op jit(solution)/shard_map/all_to_all | solution.py:134
  240.5 1.4 copy-start.1
  242.2 26.0 %copy-start.2 = (f32[512,1024]{1,0:T(8,128)S(1)}, f32[512,1024]{1,0:T(8,128)}, u32[]{:S(2)}) copy-start(f32[512,1024]{1,0:T(8,128)} %copy-done.1) | copy-start | bytes 6291460
  268.2 8.3 %copy-start.4 = (f32[1024]{0:T(1024)S(1)}, f32[1024]{0:T(1024)}, u32[]{:S(2)}) copy-start(f32[1024]{0:T(1024)} %param.23) | copy-start | bytes 12292
  268.3 8.3 %copy-start.5 = (f32[1024]{0:T(1024)S(1)}, f32[1024]{0:T(1024)}, u32[]{:S(2)}) copy-start(f32[1024]{0:T(1024)} %param.22) | copy-start | bytes 12292
  268.3 13.8 %copy-start.3 = (f32[8,1024]{1,0:T(8,128)S(1)}, f32[8,1024]{1,0:T(8,128)}, u32[]{:S(2)}) copy-start(f32[8,1024]{1,0:T(8,128)} %param.24) | copy-start | bytes 98308
  268.3 37.7 %copy-start.8 = (s32[8]{0:T(128)S(1)}, s32[8]{0:T(128)}, u32[]{:S(2)}) copy-start(s32[8]{0:T(128)} %param.25) | copy-start | bytes 100
  278.7 8.7 %all-to-all-start.3 = ((f32[8,1,1024]{2,1,0:T(1,128)}), f32[8,1,1024]{2,1,0:T(1,128)S(1)}, u32[]{:S(2)}, u32[]{:S(2)}) async-start(f32[8,1,1024]{2,1,0:T(1,128)} %broadcast_in_dim.32), calls=%async_computation.3 | async-start | bytes 65536 | tf_op jit(solution)/shard_map/all_to_all | solution.py:45
  291.4 14.5 %all-to-all-start.4 = ((bf16[16,2,512]{2,1,0:T(2,128)(2,1)}), bf16[16,2,512]{2,1,0:T(2,128)(2,1)S(1)}, u32[]{:S(2)}, u32[]{:S(2)}) async-start(bf16[16,2,512]{2,1,0:T(2,128)(2,1)} %reshape.80), calls=%async_computation.4 | async-start | bytes 65536 | tf_op jit(solution)/shard_map/all_to_all | solution.py:45
Sparse Core Ops, SparseCore 0:
  10.1 113.5 all-gather.1
where the time goes:
time: 314 us
  matrix products  167 us (53%)
  waiting for transfers between devices  49.4 us (16%)
  blocking collectives  26.9 us (9%)
  local copies, waits for them, and re-layouts  21.2 us (7%)
  starting transfers between devices  18.5 us (6%)
  between operations  15.6 us (5%)
  other arithmetic  12.1 us (4%)
    sub x4, matrix products, one_block(): expo = jnp.exp(scores - highest)  68.8 us
    dot_general x4, matrix products, one_block(): jnp.einsum('hqk,khd->qhd', probs, value_all, preferred_element_type=jnp.f...  54.7 us
    all_to_all x1, blocking collectives, several_exchanges(): lax.all_to_all(slab, axis, split_axis=0, concat_axis=0, tiled=True)  26.9 us
    dot_general x1, matrix products, expand_inner(): jnp.dot(rows_in, up_full, preferred_element_type=jnp.float32)  26 us
    all_to_all x1, waiting for transfers between devices, several_exchanges(): lax.all_to_all(slab, axis, split_axis=0, concat_axis=0, tiled=True)  21.4 us
    all_to_all x1, waiting for transfers between devices, body(): lax.all_to_all(attended, 'seq', split_axis=0, concat_axis=1, tiled=True)  15.2 us
    all_to_all x2, waiting for transfers between devices, sent_to_all(): return lax.all_to_all(copies, axis, split_axis=0, concat_axis=0, tiled=True)  12.8 us
    all_to_all x2, starting transfers between devices, sent_to_all(): return lax.all_to_all(copies, axis, split_axis=0, concat_axis=0, tiled=True)  10.3 us
  transfers between devices with their start and end apart: 5, of which 4 were waited for; matrix products, arithmetic and copies ran while one was open for 50% of the time, Pallas kernels for 0%

commit v1 on v0

--- a/solution.py
+++ b/solution.py
@@ -131,7 +131,9 @@
     projected = projected.reshape(tok_rows, 3, width)
     gathered = several_exchanges(projected, "seq", 2, 2, 0)
     attended = attend_local(gathered, length)
-    returned = lax.all_to_all(attended, "seq", split_axis=0, concat_axis=1, tiled=True)
+    cells = jnp.split(attended, lax.axis_size("seq"), axis=0)
+    received = lax.all_to_all(jnp.stack(cells), "seq", 0, 0)
+    returned = jnp.concatenate(received, axis=1)
     mixed = jnp.dot(returned, output_weight, preferred_element_type=jnp.float32)
     mixed = mixed + tokens.astype(jnp.float32)
     normed = layer_norm(mixed, first_gain, first_shift).astype(jnp.bfloat16)

time: 314 us -> 327 us (1.041)
  local copies, waits for them, and re-layouts: 21.2 us -> 33.7 us
    unnamed x21 -> x28, local copies, waits for them, and re-layouts: 2.88 us -> 13.8 us
  transfers between devices with their start and end apart: 5 -> 5, of which waited for: 4 -> 4; matrix products, arithmetic and copies ran while one was open for 50% -> 52% of each run, Pallas kernels for 0% -> 0%
where the time goes in v1:
time: 327 us; the launch traced here: 326 us
  matrix products  167 us (51%)
  waiting for transfers between devices  49.4 us (15%)
  local copies, waits for them, and re-layouts  33.7 us (10%)
  blocking collectives  26.9 us (8%)
  starting transfers between devices  18.3 us (6%)
  between operations  15.6 us (5%)
  other arithmetic  12.1 us (4%)
    sub x4, matrix products, one_block(): expo = jnp.exp(scores - highest)  68.8 us
    dot_general x4, matrix products, one_block(): jnp.einsum('hqk,khd->qhd', probs, value_all, preferred_element_type=jnp.f...  54.7 us
    all_to_all x1, blocking collectives, several_exchanges(): lax.all_to_all(slab, axis, split_axis=0, concat_axis=0, tiled=True)  26.9 us
    dot_general x1, matrix products, expand_inner(): jnp.dot(rows_in, up_full, preferred_element_type=jnp.float32)  26 us
    all_to_all x1, waiting for transfers between devices, several_exchanges(): lax.all_to_all(slab, axis, split_axis=0, concat_axis=0, tiled=True)  21.4 us
    all_to_all x1, waiting for transfers between devices, body(): received = lax.all_to_all(jnp.stack(cells), 'seq', 0, 0)  15.2 us
    unnamed x28, local copies, waits for them, and re-layouts  13.8 us
    all_to_all x2, waiting for transfers between devices, sent_to_all(): return lax.all_to_all(copies, axis, split_axis=0, concat_axis=0, tiled=True)  12.8 us
  transfers between devices with their start and end apart: 5, of which 4 were waited for; matrix products, arithmetic and copies ran while one was open for 52% of the time, Pallas kernels for 0%

profile of v1, /device:TPU:0, one launch (start us, length us, event | category | flops | bytes accessed | tf_op | source)
XLA Modules:
  0.0 326.1 jit_solution(12555600392749249684)
XLA Ops:
  7.2 2.4 pad_maximum_fusion.1
  9.6 6.6 %fusion.69 = bf16[64,8,24,128]{3,1,2,0:T(8,128)(2,1)S(1)} fusion(bf16[1024,3072]{1,0:T(8,128)(2,1)} %param.16, bf16[1,512,1024]{2,1,0:T(8,128)(2,1)} %param.14), kind=kOutput, calls=%fused_computation.84 | convolution fusion | flops 3222798336 | bytes 10485760 | tf_op jit(solution)/shard_map/dot_general | solution.py:128
  19.3 26.9 %all_to_all.26 = bf16[8,256,3,128]{3,1,2,0:T(8,128)(2,1)} all-to-all(bf16[8,256,3,128]{3,1,2,0:T(8,128)(2,1)S(1)} %get-tuple-element.88), channel_id=1, replica_groups=mesh['seq'=8,'grp'=16] {'seq'}, dimensions={0} | all-to-all | bytes 3145728 | tf_op jit(solution)/shard_map/all_to_all | solution.py:39
  46.2 4.5 %all-to-all-start.1 = ((bf16[8,256,3,128]{3,1,2,0:T(8,128)(2,1)}), bf16[8,256,3,128]{3,1,2,0:T(8,128)(2,1)}, u32[]{:S(2)}, u32[]{:S(2)}) async-start(bf16[8,256,3,128]{3,1,2,0:T(8,128)(2,1)} %get-tuple-element.89), calls=%async_computation.1 | async-start | bytes 3145728 | tf_op jit(solution)/shard_map/all_to_all | solution.py:39
  50.6 21.4 %all-to-all-done.1 = bf16[8,256,3,128]{3,1,2,0:T(8,128)(2,1)} async-done(((bf16[8,256,3,128]{3,1,2,0:T(8,128)(2,1)}), bf16[8,256,3,128]{3,1,2,0:T(8,128)(2,1)}, u32[]{:S(2)}, u32[]{:S(2)}) %all-to-all-start.1) | async-done | bytes 1572896 | tf_op jit(solution)/shard_map/all_to_all | solution.py:39
  72.0 2.2 pad_maximum_fusion
  74.5 1.6 fusion.137
  76.1 2.3 copy.46
  78.4 2.3 copy.47
  82.0 134.7 %while.11 = (s32[]{:T(128)}, bf16[4,1024,128]{2,1,0:T(8,128)(2,1)}, s32[4]{0:T(128)S(1)}, bf16[4096,2,64]{0,2,1:T(8,128)(2,1)}, bf16[4096,2,64]{0,2,1:T(8,128)(2...) while((s32[]{:T(128)}, bf16[4,1024,128]{2,1,0:T(8,128)(2,1)}, ...), condition=%wide.region_3.4_spmd.clone, body=%wide.region_0.3_spmd.clone.sunk | while | flops 2197954560 | bytes 70804144 | solution.py:89
  83.9 17.5 %fusion.162 = (f32[2,1024]{1,0:T(2,128)S(1)}, f32[2,1024,4096]{2,1,0:T(8,128)}) fusion(pred[4096]{0:T(1024)(128)(4,1)S(1)} %iota_compare_fusion.3, bf16[4096,2,64]{0,2,1:T(8,128)(2,1)} %get-tuple-element.169, bf16[4096,2,64]{0,2,1:T(8,128)(2,1)} %get-tuple-element.168, s32[]{:T(128)S(6)} %select_n.28), kind=kOutput, calls=%fused_computation.159.clone.1 | convolution fusion | flops 1107300352 | bytes 34877444 | tf_op jit(solution)/shard_map/while/body/eval_jaxpr/sub | solution.py:84
  101.4 13.9 %fusion.163 = bf16[2,1024,64]{1,2,0:T(8,128)(2,1)S(1)} fusion(bf16[4096,2,64]{0,2,1:T(8,128)(2,1)} %get-tuple-element.170, f32[2,1024,4096]{2,1,0:T(8,128)} %get-tuple-element.141, f32[2,1024]{1,0:T(2,128)S(1)} %get-tuple-element.142), kind=kOutput, calls=%fused_computation.11.clone.1 | convolution fusion | flops 1090650112 | bytes 34873344 | tf_op jit(solution)/shard_map/while/body/eval_jaxpr/hqk,khd->qhd/dot_general | solution.py:86
  118.1 17.1 %fusion.162 = (f32[2,1024]{1,0:T(2,128)S(1)}, f32[2,1024,4096]{2,1,0:T(8,128)}) fusion(pred[4096]{0:T(1024)(128)(4,1)S(1)} %iota_compare_fusion.3, bf16[4096,2,64]{0,2,1:T(8,128)(2,1)} %get-tuple-element.169, bf16[4096,2,64]{0,2,1:T(8,128)(2,1)} %get-tuple-element.168, s32[]{:T(128)S(6)} %select_n.28), kind=kOutput, calls=%fused_computation.159.clone.1 | convolution fusion | flops 1107300352 | bytes 34877444 | tf_op jit(solution)/shard_map/while/body/eval_jaxpr/sub | solution.py:84
  135.2 13.6 %fusion.163 = bf16[2,1024,64]{1,2,0:T(8,128)(2,1)S(1)} fusion(bf16[4096,2,64]{0,2,1:T(8,128)(2,1)} %get-tuple-element.170, f32[2,1024,4096]{2,1,0:T(8,128)} %get-tuple-element.141, f32[2,1024]{1,0:T(2,128)S(1)} %get-tuple-element.142), kind=kOutput, calls=%fused_computation.11.clone.1 | convolution fusion | flops 1090650112 | bytes 34873344 | tf_op jit(solution)/shard_map/while/body/eval_jaxpr/hqk,khd->qhd/dot_general | solution.py:86
  151.6 17.1 %fusion.162 = (f32[2,1024]{1,0:T(2,128)S(1)}, f32[2,1024,4096]{2,1,0:T(8,128)}) fusion(pred[4096]{0:T(1024)(128)(4,1)S(1)} %iota_compare_fusion.3, bf16[4096,2,64]{0,2,1:T(8,128)(2,1)} %get-tuple-element.169, bf16[4096,2,64]{0,2,1:T(8,128)(2,1)} %get-tuple-element.168, s32[]{:T(128)S(6)} %select_n.28), kind=kOutput, calls=%fused_computation.159.clone.1 | convolution fusion | flops 1107300352 | bytes 34877444 | tf_op jit(solution)/shard_map/while/body/eval_jaxpr/sub | solution.py:84
  168.7 13.6 %fusion.163 = bf16[2,1024,64]{1,2,0:T(8,128)(2,1)S(1)} fusion(bf16[4096,2,64]{0,2,1:T(8,128)(2,1)} %get-tuple-element.170, f32[2,1024,4096]{2,1,0:T(8,128)} %get-tuple-element.141, f32[2,1024]{1,0:T(2,128)S(1)} %get-tuple-element.142), kind=kOutput, calls=%fused_computation.11.clone.1 | convolution fusion | flops 1090650112 | bytes 34873344 | tf_op jit(solution)/shard_map/while/body/eval_jaxpr/hqk,khd->qhd/dot_general | solution.py:86
  185.1 17.1 %fusion.162 = (f32[2,1024]{1,0:T(2,128)S(1)}, f32[2,1024,4096]{2,1,0:T(8,128)}) fusion(pred[4096]{0:T(1024)(128)(4,1)S(1)} %iota_compare_fusion.3, bf16[4096,2,64]{0,2,1:T(8,128)(2,1)} %get-tuple-element.169, bf16[4096,2,64]{0,2,1:T(8,128)(2,1)} %get-tuple-element.168, s32[]{:T(128)S(6)} %select_n.28), kind=kOutput, calls=%fused_computation.159.clone.1 | convolution fusion | flops 1107300352 | bytes 34877444 | tf_op jit(solution)/shard_map/while/body/eval_jaxpr/sub | solution.py:84
  202.2 13.6 %fusion.163 = bf16[2,1024,64]{1,2,0:T(8,128)(2,1)S(1)} fusion(bf16[4096,2,64]{0,2,1:T(8,128)(2,1)} %get-tuple-element.170, f32[2,1024,4096]{2,1,0:T(8,128)} %get-tuple-element.141, f32[2,1024]{1,0:T(2,128)S(1)} %get-tuple-element.142), kind=kOutput, calls=%fused_computation.11.clone.1 | convolution fusion | flops 1090650112 | bytes 34873344 | tf_op jit(solution)/shard_map/while/body/eval_jaxpr/hqk,khd->qhd/dot_general | solution.py:86
  216.7 1.6 fusion.96
  218.3 1.6 fusion.95
  219.9 1.6 fusion.94
  223.0 1.6 fusion.92
  227.7 1.6 fusion.89
  229.3 3.6 %all-to-all-start.2 = ((bf16[8,512,128]{2,1,0:T(8,128)(2,1)}), bf16[8,512,128]{2,1,0:T(8,128)(2,1)S(1)}, u32[]{:S(2)}, u32[]{:S(2)}) async-start(bf16[8,512,128]{2,1,0:T(8,128)(2,1)} %fusion.89), calls=%async_computation.2 | async-start | bytes 2097152 | tf_op jit(solution)/shard_map/all_to_all | solution.py:135
  233.5 15.2 %all-to-all-done.2 = bf16[8,512,128]{2,1,0:T(8,128)(2,1)S(1)} async-done(((bf16[8,512,128]{2,1,0:T(8,128)(2,1)}), bf16[8,512,128]{2,1,0:T(8,128)(2,1)S(1)}, u32[]{:S(2)}, u32[]{:S(2)}) %all-to-all-start.2) | async-done | bytes 1048608 | tf_op jit(solution)/shard_map/all_to_all | solution.py:135
  250.0 2.9 fusion.139
  254.6 26.0 %fusion.73.clone.5 = bf16[512,4096]{1,0:T(8,128)(2,1)S(1)} fusion(bf16[1024,8192]{1,0:T(8,128)(2,1)} %all-gather.2.cloned.1.call-done, f32[512,1024]{1,0:T(8,128)} %copy-done.1, f32[1024]{0:T(1024)S(1)} %copy-done.6, f32[1024]{0:T(1024)S(1)} %copy-done.7, f32[512]{0:T(512)S(1)} %add_rsqrt_fusion.1, ...), kind=kOutput, calls=%fused_computation.24.clone.clone.clone.clone.clone.clone.2 | convolution fusion | flops 4433903616 | bytes 14692352 | tf_op jit(solution)/shard_map/dot_general | solution.py:99
  280.7 7.9 %fusion.140 = (f32[512]{0:T(512)S(1)}, f32[512,1024]{1,0:T(8,128)S(1)}) fusion(f32[1024]{0:T(1024)S(1)} %copy-done.6, f32[1024]{0:T(1024)S(1)} %copy-done.7, f32[512]{0:T(512)S(1)} %add_rsqrt_fusion.1, f32[512,1024]{1,0:T(8,128)S(1)} %copy-done.2, f32[512]{0:T(512)S(1)} %broadcast_multiply_fusion.1, bf16[1024,8192]{1,0:T(8,128)(2,1)} %all-gather.2.cloned.1.call-done, ...), kind=kOutput, calls=%fused_computation.163 | convolution fusion | flops 4299161088 | bytes 16791552 | tf_op jit(solution)/shard_map/dot_general | solution.py:104
  291.1 3.3 %all-to-all-start.3 = ((f32[8,1,1024]{2,1,0:T(1,128)}), f32[8,1,1024]{2,1,0:T(1,128)S(1)}, u32[]{:S(2)}, u32[]{:S(2)}) async-start(f32[8,1,1024]{2,1,0:T(1,128)} %broadcast_in_dim.32), calls=%async_computation.3 | async-start | bytes 65536 | tf_op jit(solution)/shard_map/all_to_all | solution.py:45
  294.6 5.2 %all-to-all-done.3 = f32[8,1,1024]{2,1,0:T(1,128)S(1)} async-done(((f32[8,1,1024]{2,1,0:T(1,128)}), f32[8,1,1024]{2,1,0:T(1,128)S(1)}, u32[]{:S(2)}, u32[]{:S(2)}) %all-to-all-start.3) | async-done | bytes 32800 | tf_op jit(solution)/shard_map/all_to_all | solution.py:45
  303.8 6.9 %all-to-all-start.4 = ((bf16[16,2,512]{2,1,0:T(2,128)(2,1)}), bf16[16,2,512]{2,1,0:T(2,128)(2,1)S(1)}, u32[]{:S(2)}, u32[]{:S(2)}) async-start(bf16[16,2,512]{2,1,0:T(2,128)(2,1)} %reshape.87), calls=%async_computation.4 | async-start | bytes 65536 | tf_op jit(solution)/shard_map/all_to_all | solution.py:45
  310.7 7.6 %all-to-all-done.4 = bf16[16,2,512]{2,1,0:T(2,128)(2,1)S(1)} async-done(((bf16[16,2,512]{2,1,0:T(2,128)(2,1)}), bf16[16,2,512]{2,1,0:T(2,128)(2,1)S(1)}, u32[]{:S(2)}, u32[]{:S(2)}) %all-to-all-start.4) | async-done | bytes 32800 | tf_op jit(solution)/shard_map/all_to_all | solution.py:45
  (69 shorter events, 27.7 us)
Async XLA Ops:
  7.2 242.8 %copy-start = (bf16[1024,1024]{1,0:T(8,128)(2,1)S(1)}, bf16[1024,1024]{1,0:T(8,128)(2,1)}, u32[]{:S(2)}) copy-start(bf16[1024,1024]{1,0:T(8,128)(2,1)} %param.17) | copy-start | bytes 6291460
  7.2 247.4 %all-gather.2.cloned.1.call-start = ((), (), s32[]{:S(2)}) async-start(), calls=%async_computation.5 | async-start | bytes 17825792 | tf_op jit(solution)/shard_map/all_gather | solution.py:13
  46.2 25.9 %all-to-all-start.1 = ((bf16[8,256,3,128]{3,1,2,0:T(8,128)(2,1)}), bf16[8,256,3,128]{3,1,2,0:T(8,128)(2,1)}, u32[]{:S(2)}, u32[]{:S(2)}) async-start(bf16[8,256,3,128]{3,1,2,0:T(8,128)(2,1)} %get-tuple-element.89), calls=%async_computation.1 | async-start | bytes 3145728 | tf_op jit(solution)/shard_map/all_to_all | solution.py:39
  216.7 37.9 %copy-start.6 = (f32[1024]{0:T(1024)S(1)}, f32[1024]{0:T(1024)}, u32[]{:S(2)}) copy-start(f32[1024]{0:T(1024)} %param.19) | copy-start | bytes 12292
  216.7 37.9 %copy-start.7 = (f32[1024]{0:T(1024)S(1)}, f32[1024]{0:T(1024)}, u32[]{:S(2)}) copy-start(f32[1024]{0:T(1024)} %param.18) | copy-start | bytes 12292
  229.3 19.4 %all-to-all-start.2 = ((bf16[8,512,128]{2,1,0:T(8,128)(2,1)}), bf16[8,512,128]{2,1,0:T(8,128)(2,1)S(1)}, u32[]{:S(2)}, u32[]{:S(2)}) async-start(bf16[8,512,128]{2,1,0:T(8,128)(2,1)} %fusion.89), calls=%async_computation.2 | async-start | bytes 2097152 | tf_op jit(solution)/shard_map/all_to_all | solution.py:135
  252.9 1.4 copy-start.1
  254.6 26.0 %copy-start.2 = (f32[512,1024]{1,0:T(8,128)S(1)}, f32[512,1024]{1,0:T(8,128)}, u32[]{:S(2)}) copy-start(f32[512,1024]{1,0:T(8,128)} %copy-done.1) | copy-start | bytes 6291460
  280.6 8.3 %copy-start.4 = (f32[1024]{0:T(1024)S(1)}, f32[1024]{0:T(1024)}, u32[]{:S(2)}) copy-start(f32[1024]{0:T(1024)} %param.23) | copy-start | bytes 12292
  280.6 8.3 %copy-start.5 = (f32[1024]{0:T(1024)S(1)}, f32[1024]{0:T(1024)}, u32[]{:S(2)}) copy-start(f32[1024]{0:T(1024)} %param.22) | copy-start | bytes 12292
  280.7 13.8 %copy-start.3 = (f32[8,1024]{1,0:T(8,128)S(1)}, f32[8,1024]{1,0:T(8,128)}, u32[]{:S(2)}) copy-start(f32[8,1024]{1,0:T(8,128)} %param.24) | copy-start | bytes 98308
  280.7 37.7 %copy-start.8 = (s32[8]{0:T(128)S(1)}, s32[8]{0:T(128)}, u32[]{:S(2)}) copy-start(s32[8]{0:T(128)} %param.25) | copy-start | bytes 100
  291.1 8.7 %all-to-all-start.3 = ((f32[8,1,1024]{2,1,0:T(1,128)}), f32[8,1,1024]{2,1,0:T(1,128)S(1)}, u32[]{:S(2)}, u32[]{:S(2)}) async-start(f32[8,1,1024]{2,1,0:T(1,128)} %broadcast_in_dim.32), calls=%async_computation.3 | async-start | bytes 65536 | tf_op jit(solution)/shard_map/all_to_all | solution.py:45
  303.8 14.5 %all-to-all-start.4 = ((bf16[16,2,512]{2,1,0:T(2,128)(2,1)}), bf16[16,2,512]{2,1,0:T(2,128)(2,1)S(1)}, u32[]{:S(2)}, u32[]{:S(2)}) async-start(bf16[16,2,512]{2,1,0:T(2,128)(2,1)} %reshape.87), calls=%async_computation.4 | async-start | bytes 65536 | tf_op jit(solution)/shard_map/all_to_all | solution.py:45
Sparse Core Ops, SparseCore 0:
  10.1 113.5 all-gather.1
